TPU v7x, 32 devices: a whole 2x2x4 slice. The times are simulated.
32 devices in a mesh: dp: 4 (over y, x), row: 4 (over z), col: 2 (over core).
Axes of the slice: x: 2, y: 2, z: 4, core: 2. Of those that a mesh axis runs over, the one named last changes fastest.
Arguments:
- activations: bfloat16 [4, 64, 128, 512], P('dp', None, 'row', 'col'), may hold values from -18 to 18
- kernel: bfloat16 [3, 3, 64, 64], replicated, may hold values from -0.125 to 0.125
- gain: float32 [64], replicated, may hold values from 0.25 to 1.75
- cotangent: bfloat16 [4, 64, 128, 512], P('dp', None, 'row', 'col'), may hold values from -16 to 16
Outputs:
- input_grad: bfloat16 [4, 64, 128, 512], P('dp', None, 'row', 'col')
- weight_grad: float32 [3, 3, 64, 64], P(None, None, 'dp')
- gain_grad: float32 [64], replicated
- shift_grad: float32 [64], replicated
All inputs are finite; a program needn't handle non-finite values.
Results may differ from a plain program's by a relative error of at most 0.0049.
Values may be sent and summed in bfloat16 or wider, within the bound.
A program may use at most 64 MiB of HBM per device.

v0:
```python
import jax
import jax.numpy as jnp
from jax import lax
from jax.sharding import PartitionSpec as P


def with_halo(shard, sides, width):
    for axis, dim in sides:
        count, length = (lax.axis_size(axis), shard.shape[dim])
        up = [(i, (i + 1) % count) for i in range(count - 1)]
        down = [(j, i) for i, j in up]
        last = lax.slice_in_dim(shard, length - width, length, axis=dim)
        initial = lax.slice_in_dim(shard, 0, width, axis=dim)
        before = lax.ppermute(last, axis, up)
        after = lax.ppermute(initial, axis, down)
        shard = jnp.concatenate([before, shard, after], axis=dim)
    return shard


def per_device(activations, kernel, gain, cotangent):
    images, channels, height, width = activations.shape
    total = jnp.float32(
        images * height * width * lax.axis_size("dp") * lax.axis_size("row") * lax.axis_size("col")
    )
    padded = with_halo(activations, (("row", 2), ("col", 3)), 1)
    pre = jnp.zeros((images, channels, height, width), jnp.float32)
    for tap_row in range(3):
        for tap_col in range(3):
            window = padded[:, :, tap_row : tap_row + height, tap_col : tap_col + width]
            pre = pre + jnp.einsum(
                "oc,bchw->bohw",
                kernel[tap_row, tap_col],
                window,
                preferred_element_type=jnp.float32,
            )
    grad = cotangent.astype(jnp.float32)
    local_pre = jnp.sum(pre, axis=(0, 2, 3))
    local_sq = jnp.sum(pre * pre, axis=(0, 2, 3))
    local_cot = jnp.sum(grad, axis=(0, 2, 3))
    local_cross = jnp.sum(grad * pre, axis=(0, 2, 3))
    sum_pre, sum_sq, sum_cot, sum_cross = lax.psum(
        (local_pre, local_sq, local_cot, local_cross), ("dp", "row", "col")
    )
    mean = sum_pre / total
    rstd = lax.rsqrt(sum_sq / total - mean * mean + 1e-05)
    sum_norm = (sum_cross - mean * sum_cot) * rstd
    normed = (pre - mean[:, None, None]) * rstd[:, None, None]
    pre_grad = (gain * rstd)[:, None, None] * (
        grad - (sum_cot / total)[:, None, None] - normed * (sum_norm / total)[:, None, None]
    )
    pre_grad = pre_grad.astype(jnp.bfloat16)
    grad_padded = with_halo(pre_grad, (("row", 2), ("col", 3)), 1)
    input_grad = jnp.zeros((images, channels, height, width), jnp.float32)
    kernel_terms = []
    for tap_row in range(3):
        for tap_col in range(3):
            shifted = grad_padded[
                :, :, 2 - tap_row : 2 - tap_row + height, 2 - tap_col : 2 - tap_col + width
            ]
            input_grad = input_grad + jnp.einsum(
                "oc,bohw->bchw",
                kernel[tap_row, tap_col],
                shifted,
                preferred_element_type=jnp.float32,
            )
            window = padded[:, :, tap_row : tap_row + height, tap_col : tap_col + width]
            kernel_terms.append(
                jnp.einsum("bohw,bchw->oc", pre_grad, window, preferred_element_type=jnp.float32)
            )
    factor = total ** (-0.5)
    local_kernel = jnp.stack(kernel_terms).reshape(3, 3, channels, channels) * factor
    spatial = lax.psum(local_kernel, ("row", "col"))
    weight_grad = lax.psum_scatter(spatial, "dp", scatter_dimension=2, tiled=True)
    return (input_grad.astype(jnp.bfloat16), weight_grad, sum_norm / total, sum_cot / total)


def solution(mesh):
    return jax.shard_map(
        per_device,
        mesh=mesh,
        in_specs=(P("dp", None, "row", "col"), P(), P(), P("dp", None, "row", "col")),
        out_specs=(P("dp", None, "row", "col"), P(None, None, "dp", None), P(), P()),
        check_vma=False,
    )
```

profile of v0, /device:TPU:0, one launch (start us, length us, event | category | flops | bytes accessed | tf_op | source)
XLA Modules:
  0.0 162.4 jit_solution(4085869104326707929)
XLA Ops:
  7.2 1.9 %copy.26 = bf16[1,64,32,256]{3,1,2,0:T(8,128)(2,1)S(1)} copy(bf16[1,64,32,256]{3,2,1,0:T(8,128)(2,1)} %param.4) | data formatting | bytes 2097152 | tf_op args[0]
  9.2 5.0 %collective-permute-start = (bf16[1,64,1,256]{3,1,2,0:T(8,128)(2,1)S(1)}, bf16[1,64,1,256]{3,1,2,0:T(8,128)(2,1)S(1)}, u32[]{:S(2)}, u32[]{:S(2)}) collective-permute-start(bf16[1,64,1,256]{3,1,2,0:T(8,128)(2,1)S(1)} %get-tuple-element.29), channel_id=1, source_target_pairs={{0,2},{2,4},{4,6},{1,3},{3,5},{5,7},{8,10},{10,12},{12,14},{9,11},... | collective-permute-start | bytes 98312 | tf_op jit(solution)/shard_map/ppermute | solution.py:14
  14.1 1.3 collective-permute-start.1
  15.4 2.2 %fusion.55 = f32[32,256,64]{1,2,0:T(8,128)} fusion(bf16[64,32,256]{2,1,0:T(8,128)(2,1)S(1)} %bitcast.222, bf16[3,3,64,64]{3,2,1,0:T(8,128)(2,1)S(1)} %copy-done.18), kind=kOutput, calls=%fused_computation.92 | convolution fusion | flops 67108864 | bytes 3162112 | tf_op jit(solution)/shard_map/oc,bchw->bohw/dot_general | solution.py:30
  18.3 1.7 %collective-permute-done.1 = bf16[1,64,1,256]{3,1,2,0:T(8,128)(2,1)S(1)} collective-permute-done((bf16[1,64,1,256]{3,1,2,0:T(8,128)(2,1)S(1)}, bf16[1,64,1,256]{3,1,2,0:T(8,128)(2,1)S(1)}, u32[]{:S(2)}, u32[]{:S(2)}) %collective-permute-start.1) | collective-permute-done | bytes 32800 | tf_op jit(solution)/shard_map/ppermute | solution.py:15
  22.2 3.0 %collective-permute-start.2 = (bf16[1,64,34,1]{1,2,3,0:T(8,128)(2,1)S(1)}, bf16[1,64,34,1]{1,2,3,0:T(8,128)(2,1)S(1)}, u32[]{:S(2)}, u32[]{:S(2)}) collective-permute-start(bf16[1,64,34,1]{1,2,3,0:T(8,128)(2,1)S(1)} %copy.29), channel_id=1, source_target_pairs={{0,1},{2,3},{4,5},{6,7},{8,9},{10,11},{12,13},{14,15},{16,17},{18,... | collective-permute-start | bytes 13064 | tf_op jit(solution)/shard_map/ppermute | solution.py:14
  25.2 1.8 %fusion.58 = f32[32,256,64]{1,2,0:T(8,128)} fusion(bf16[1,64,32,256]{3,1,2,0:T(8,128)(2,1)S(1)} %copy.26, bf16[1,64,1,256]{3,1,2,0:T(8,128)(2,1)S(1)} %collective-permute-done, bf16[3,3,64,64]{3,2,1,0:T(8,128)(2,1)S(1)} %copy-done.18), kind=kOutput, calls=%fused_computation.94 | convolution fusion | flops 69206016 | bytes 3194880 | tf_op jit(solution)/shard_map/oc,bchw->bohw/dot_general | solution.py:30
  27.0 1.7 %fusion.61 = f32[32,256,64]{1,2,0:T(8,128)} fusion(bf16[1,64,1,256]{3,1,2,0:T(8,128)(2,1)S(1)} %collective-permute-done.1, bf16[1,64,32,256]{3,1,2,0:T(8,128)(2,1)S(1)} %copy.26, bf16[3,3,64,64]{3,2,1,0:T(8,128)(2,1)S(1)} %copy-done.18), kind=kOutput, calls=%fused_computation.95 | convolution fusion | flops 69206016 | bytes 3194880 | tf_op jit(solution)/shard_map/oc,bchw->bohw/dot_general | solution.py:30
  29.1 2.1 %fusion.78 = f32[32,256,64]{1,2,0:T(8,128)} fusion(bf16[3,3,64,64]{3,2,1,0:T(8,128)(2,1)S(1)} %copy-done.18, bf16[1,64,34,256]{3,1,2,0:T(8,128)(2,1)S(1)} %constant_dynamic-update-slice_fusion, bf16[1,64,34,1]{3,1,2,0:T(8,128)(2,1)S(1)} %copy.33), kind=kOutput, calls=%fused_computation.109 | convolution fusion | flops 69206016 | bytes 3784704 | tf_op jit(solution)/shard_map/oc,bchw->bohw/dot_general | solution.py:30
  31.1 2.1 %fusion.86 = f32[32,256,64]{1,2,0:T(8,128)} fusion(bf16[3,3,64,64]{3,2,1,0:T(8,128)(2,1)S(1)} %copy-done.18, bf16[1,64,34,256]{3,1,2,0:T(8,128)(2,1)S(1)} %constant_dynamic-update-slice_fusion, bf16[1,64,34,1]{3,1,2,0:T(8,128)(2,1)S(1)} %copy.33), kind=kOutput, calls=%fused_computation.117 | convolution fusion | flops 69206016 | bytes 3784704 | tf_op jit(solution)/shard_map/oc,bchw->bohw/dot_general | solution.py:30
  38.3 3.8 %fusion.3 = (f32[64]{0:T(128)S(1)}, f32[64]{0:T(128)S(1)}, f32[64]{0:T(128)S(1)}, f32[32,256,64]{1,2,0:T(8,128)S(1)}) fusion(bf16[1,64,32,256]{3,2,1,0:T(8,128)(2,1)} %param.7, bf16[1,64,34,1]{3,1,2,0:T(8,128)(2,1)S(1)} %copy-done.2, bf16[1,64,34,256]{3,1,2,0:T(8,128)(2,1)S(1)} %constant_dynamic-update-slice_fusion, ...), kind=kOutput, calls=%fused_computation.6 | convolution fusion | flops 76545856 | bytes 21611264 | tf_op jit(solution)/shard_map/oc,bchw->bohw/dot_general | solution.py:30
  42.3 40.6 %all-reduce = (f32[64]{0:T(128)S(1)}, f32[64]{0:T(128)S(1)}, f32[64]{0:T(128)S(1)}, f32[64]{0:T(128)S(1)}) all-reduce(f32[64]{0:T(128)S(1)} %get-tuple-element.13, f32[64]{0:T(128)S(1)} %reduce_sum.37, f32[64]{0:T(128)S(1)} %get-tuple-element.12, f32[64]{0:T(128)S(1)} %get-tuple-element.14), channel_id=1, replica_groups=mesh['dp'=4,'row'=4,'col'=2] {'dp','row','col'}, use_global_device_ids=true, to_apply=%region_1.0 | all-reduce | flops 256 | bytes 2048 | tf_op jit(solution)/shard_map/psum | solution.py:41
  83.0 2.8 %fusion.2 = bf16[1,64,32,256]{3,1,2,0:T(8,128)(2,1)S(1)} fusion(f32[32,256,64]{1,2,0:T(8,128)} %copy-done, f32[64]{0:T(128)S(1)} %get-tuple-element.32, f32[64]{0:T(128)S(1)} %get-tuple-element.20, f32[64]{0:T(128)S(1)} %get-tuple-element.33, f32[64]{0:T(128)S(1)} %get-tuple-element.31, f32[64]{0:T(128)S(1)} %get-tuple-element.19, ...), kind=kLoop, calls=%fused_computation.5 | loop fusion | flops 4194304 | bytes 4195584 | tf_op jit(solution)/shard_map/convert_element_type | solution.py:51
  86.4 1.8 %fusion.52 = f32[32,256,64]{1,2,0:T(8,128)} fusion(bf16[1,64,32,256]{3,1,2,0:T(8,128)(2,1)S(1)} %fusion.2, bf16[3,3,64,64]{3,2,1,0:T(8,128)(2,1)S(1)} %copy-done.18), kind=kOutput, calls=%fused_computation.89 | convolution fusion | flops 67108864 | bytes 3162112 | tf_op jit(solution)/shard_map/oc,bohw->bchw/dot_general | solution.py:60
  91.2 1.3 fusion.11
  96.3 4.5 %collective-permute-start.4 = (bf16[1,64,1,256]{3,1,2,0:T(8,128)(2,1)S(1)}, bf16[1,64,1,256]{3,1,2,0:T(8,128)(2,1)S(1)}, u32[]{:S(2)}, u32[]{:S(2)}) collective-permute-start(bf16[1,64,1,256]{3,1,2,0:T(8,128)(2,1)S(1)} %get-tuple-element.28), channel_id=1, source_target_pairs={{0,2},{2,4},{4,6},{1,3},{3,5},{5,7},{8,10},{10,12},{12,14},{9,11},... | collective-permute-start | bytes 98312 | tf_op jit(solution)/shard_map/ppermute | solution.py:14
  104.8 3.2 %collective-permute-start.7 = (bf16[1,64,34,1]{1,2,3,0:T(8,128)(2,1)S(1)}, bf16[1,64,34,1]{1,2,3,0:T(8,128)(2,1)S(1)}, u32[]{:S(2)}, u32[]{:S(2)}) collective-permute-start(bf16[1,64,34,1]{1,2,3,0:T(8,128)(2,1)S(1)} %copy.41), channel_id=1, source_target_pairs={{0,1},{2,3},{4,5},{6,7},{8,9},{10,11},{12,13},{14,15},{16,17},{18,... | collective-permute-start | bytes 13064 | tf_op jit(solution)/shard_map/ppermute | solution.py:14
  108.1 1.8 %fusion.35 = f32[32,256,64]{1,2,0:T(8,128)} fusion(bf16[1,64,1,256]{3,1,2,0:T(8,128)(2,1)S(1)} %collective-permute-done.5, bf16[1,64,32,256]{3,1,2,0:T(8,128)(2,1)S(1)} %fusion.2, bf16[3,3,64,64]{3,2,1,0:T(8,128)(2,1)S(1)} %copy-done.18), kind=kOutput, calls=%fused_computation.68 | convolution fusion | flops 67633152 | bytes 3194880 | tf_op jit(solution)/shard_map/oc,bohw->bchw/dot_general | solution.py:60
  109.9 1.8 %fusion.27 = f32[32,256,64]{1,2,0:T(8,128)} fusion(bf16[1,64,32,256]{3,1,2,0:T(8,128)(2,1)S(1)} %fusion.2, bf16[1,64,1,256]{3,1,2,0:T(8,128)(2,1)S(1)} %collective-permute-done.4, bf16[3,3,64,64]{3,2,1,0:T(8,128)(2,1)S(1)} %copy-done.18), kind=kOutput, calls=%fused_computation.56 | convolution fusion | flops 67633152 | bytes 3194880 | tf_op jit(solution)/shard_map/oc,bohw->bchw/dot_general | solution.py:60
  112.5 1.4 maximum_maximum_fusion
  118.5 1.6 fusion.24
  120.1 1.6 copy.51
  121.6 3.8 %reduce-scatter.2.cloned.1.call-done = f32[3,3,16,64]{3,2,1,0:T(8,128)} async-done(((f32[3,3,64,64]{3,2,1,0:T(8,128)}), f32[3,3,16,64]{3,2,1,0:T(8,128)}) %reduce-scatter.2.cloned.1.call-update) | async-done | bytes 36880 | tf_op jit(solution)/shard_map/reduce_scatter | solution.py:73
  125.5 30.0 %psum.40 = f32[3,3,16,64]{3,2,1,0:T(8,128)} all-reduce(f32[3,3,16,64]{3,2,1,0:T(8,128)} %reduce-scatter.2.cloned.1.call-done), channel_id=1, replica_groups=mesh['dp'=4,'row'=4,'col'=2] {'row','col'}, use_global_device_ids=true, to_apply=%region_8.0 | all-reduce | flops 9216 | bytes 73728 | tf_op jit(solution)/shard_map/psum | solution.py:72
  (92 shorter events, 24.9 us)
Async XLA Ops:
  7.2 8.3 %copy-start.8 = (bf16[1,64,32,256]{3,2,1,0:T(8,128)(2,1)S(1)}, bf16[1,64,32,256]{3,2,1,0:T(8,128)(2,1)}, u32[]{:S(2)}) copy-start(bf16[1,64,32,256]{3,2,1,0:T(8,128)(2,1)} %param.4) | copy-start | bytes 3145732
  7.2 8.3 %copy-start.18 = (bf16[3,3,64,64]{3,2,1,0:T(8,128)(2,1)S(1)}, bf16[3,3,64,64]{3,2,1,0:T(8,128)(2,1)}, u32[]{:S(2)}) copy-start(bf16[3,3,64,64]{3,2,1,0:T(8,128)(2,1)} %param.5) | copy-start | bytes 221188
  7.2 118.3 %reduce-scatter.2.cloned.1.call-start = ((), (), s32[]{:S(2)}) async-start(), calls=%async_computation.1 | async-start | bytes 368640 | tf_op jit(solution)/shard_map/reduce_scatter | solution.py:73
  9.1 17.8 %copy-start.6 = (bf16[1,64,32,256]{3,1,2,0:T(8,128)(2,1)}, bf16[1,64,32,256]{3,1,2,0:T(8,128)(2,1)S(1)}, u32[]{:S(2)}) copy-start(bf16[1,64,32,256]{3,1,2,0:T(8,128)(2,1)S(1)} %copy.26) | copy-start | bytes 3145732
  9.2 8.5 %collective-permute-start = (bf16[1,64,1,256]{3,1,2,0:T(8,128)(2,1)S(1)}, bf16[1,64,1,256]{3,1,2,0:T(8,128)(2,1)S(1)}, u32[]{:S(2)}, u32[]{:S(2)}) collective-permute-start(bf16[1,64,1,256]{3,1,2,0:T(8,128)(2,1)S(1)} %get-tuple-element.29), channel_id=1, source_target_pairs={{0,2},{2,4},{4,6},{1,3},{3,5},{5,7},{8,10},{10,12},{12,14},{9,11},... | collective-permute-start | bytes 98312 | tf_op jit(solution)/shard_map/ppermute | solution.py:14
  14.1 5.8 %collective-permute-start.1 = (bf16[1,64,1,256]{3,1,2,0:T(8,128)(2,1)S(1)}, bf16[1,64,1,256]{3,1,2,0:T(8,128)(2,1)S(1)}, u32[]{:S(2)}, u32[]{:S(2)}) collective-permute-start(bf16[1,64,1,256]{3,1,2,0:T(8,128)(2,1)S(1)} %get-tuple-element.30), channel_id=1, source_target_pairs={{2,0},{4,2},{6,4},{3,1},{5,3},{7,5},{10,8},{12,10},{14,12},{11,9},... | collective-permute-start | bytes 98312 | tf_op jit(solution)/shard_map/ppermute | solution.py:15
  20.6 8.1 %collective-permute-start.3 = (bf16[1,64,34,1]{1,2,3,0:T(8,128)(2,1)S(1)}, bf16[1,64,34,1]{1,2,3,0:T(8,128)(2,1)S(1)}, u32[]{:S(2)}, u32[]{:S(2)}) collective-permute-start(bf16[1,64,34,1]{1,2,3,0:T(8,128)(2,1)S(1)} %copy.32), channel_id=1, source_target_pairs={{1,0},{3,2},{5,4},{7,6},{9,8},{11,10},{13,12},{15,14},{17,16},{19,... | collective-permute-start | bytes 13064 | tf_op jit(solution)/shard_map/ppermute | solution.py:15
  22.2 11.0 %collective-permute-start.2 = (bf16[1,64,34,1]{1,2,3,0:T(8,128)(2,1)S(1)}, bf16[1,64,34,1]{1,2,3,0:T(8,128)(2,1)S(1)}, u32[]{:S(2)}, u32[]{:S(2)}) collective-permute-start(bf16[1,64,34,1]{1,2,3,0:T(8,128)(2,1)S(1)} %copy.29), channel_id=1, source_target_pairs={{0,1},{2,3},{4,5},{6,7},{8,9},{10,11},{12,13},{14,15},{16,17},{18,... | collective-permute-start | bytes 13064 | tf_op jit(solution)/shard_map/ppermute | solution.py:14
  29.1 4.2 %copy-start.1 = (bf16[1,64,34,1]{3,1,2,0:T(8,128)(2,1)}, bf16[1,64,34,1]{3,1,2,0:T(8,128)(2,1)S(1)}, u32[]{:S(2)}) copy-start(bf16[1,64,34,1]{3,1,2,0:T(8,128)(2,1)S(1)} %copy.33) | copy-start | bytes 13060
  33.6 2.4 %copy-start.17 = (f32[32,256,64]{1,2,0:T(8,128)S(1)}, f32[32,256,64]{1,2,0:T(8,128)}, u32[]{:S(2)}) copy-start(f32[32,256,64]{1,2,0:T(8,128)} %fusion.86) | copy-start | bytes 6291460
  34.2 2.6 %copy-start.14 = (f32[32,256,64]{1,2,0:T(8,128)S(1)}, f32[32,256,64]{1,2,0:T(8,128)}, u32[]{:S(2)}) copy-start(f32[32,256,64]{1,2,0:T(8,128)} %fusion.58) | copy-start | bytes 6291460
  34.2 3.2 %copy-start.15 = (f32[32,256,64]{1,2,0:T(8,128)S(1)}, f32[32,256,64]{1,2,0:T(8,128)}, u32[]{:S(2)}) copy-start(f32[32,256,64]{1,2,0:T(8,128)} %fusion.61) | copy-start | bytes 6291460
  34.8 2.7 %copy-start.2 = (bf16[1,64,34,1]{3,1,2,0:T(8,128)(2,1)S(1)}, bf16[1,64,34,1]{3,1,2,0:T(8,128)(2,1)}, u32[]{:S(2)}) copy-start(bf16[1,64,34,1]{3,1,2,0:T(8,128)(2,1)} %copy-done.1) | copy-start | bytes 13060
  34.8 3.5 %copy-start.11 = (f32[32,256,64]{1,2,0:T(8,128)S(1)}, f32[32,256,64]{1,2,0:T(8,128)}, u32[]{:S(2)}) copy-start(f32[32,256,64]{1,2,0:T(8,128)} %fusion.55) | copy-start | bytes 6291460
  42.1 40.9 %copy-start = (f32[32,256,64]{1,2,0:T(8,128)}, f32[32,256,64]{1,2,0:T(8,128)S(1)}, u32[]{:S(2)}) copy-start(f32[32,256,64]{1,2,0:T(8,128)S(1)} %get-tuple-element.34) | copy-start | bytes 6291460
  42.1 40.9 %copy-start.21 = (f32[64]{0:T(128)S(1)}, f32[64]{0:T(128)}, u32[]{:S(2)}) copy-start(f32[64]{0:T(128)} %param.6) | copy-start | bytes 772
  83.0 2.8 %copy-start.19 = (f32[64]{0:T(128)}, f32[64]{0:T(128)S(1)}, u32[]{:S(2)}) copy-start(f32[64]{0:T(128)S(1)} %get-tuple-element.31) | copy-start | bytes 772
  83.0 2.8 %copy-start.20 = (f32[64]{0:T(128)}, f32[64]{0:T(128)S(1)}, u32[]{:S(2)}) copy-start(f32[64]{0:T(128)S(1)} %get-tuple-element.32) | copy-start | bytes 772
  83.0 2.8 %copy-start.5 = (bf16[1,64,34,1]{3,1,2,0:T(8,128)(2,1)S(1)}, bf16[1,64,34,1]{3,1,2,0:T(8,128)(2,1)}, u32[]{:S(2)}) copy-start(bf16[1,64,34,1]{3,1,2,0:T(8,128)(2,1)} %copy-done.4) | copy-start | bytes 13060
  95.0 6.6 %collective-permute-start.5 = (bf16[1,64,1,256]{3,1,2,0:T(8,128)(2,1)S(1)}, bf16[1,64,1,256]{3,1,2,0:T(8,128)(2,1)S(1)}, u32[]{:S(2)}, u32[]{:S(2)}) collective-permute-start(bf16[1,64,1,256]{3,1,2,0:T(8,128)(2,1)S(1)} %get-tuple-element.27), channel_id=1, source_target_pairs={{2,0},{4,2},{6,4},{3,1},{5,3},{7,5},{10,8},{12,10},{14,12},{11,9},... | collective-permute-start | bytes 98312 | tf_op jit(solution)/shard_map/ppermute | solution.py:15
  96.3 6.1 %collective-permute-start.4 = (bf16[1,64,1,256]{3,1,2,0:T(8,128)(2,1)S(1)}, bf16[1,64,1,256]{3,1,2,0:T(8,128)(2,1)S(1)}, u32[]{:S(2)}, u32[]{:S(2)}) collective-permute-start(bf16[1,64,1,256]{3,1,2,0:T(8,128)(2,1)S(1)} %get-tuple-element.28), channel_id=1, source_target_pairs={{0,2},{2,4},{4,6},{1,3},{3,5},{5,7},{8,10},{10,12},{12,14},{9,11},... | collective-permute-start | bytes 98312 | tf_op jit(solution)/shard_map/ppermute | solution.py:14
  103.2 8.5 %collective-permute-start.6 = (bf16[1,64,34,1]{1,2,3,0:T(8,128)(2,1)S(1)}, bf16[1,64,34,1]{1,2,3,0:T(8,128)(2,1)S(1)}, u32[]{:S(2)}, u32[]{:S(2)}) collective-permute-start(bf16[1,64,34,1]{1,2,3,0:T(8,128)(2,1)S(1)} %copy.37), channel_id=1, source_target_pairs={{1,0},{3,2},{5,4},{7,6},{9,8},{11,10},{13,12},{15,14},{17,16},{19,... | collective-permute-start | bytes 13064 | tf_op jit(solution)/shard_map/ppermute | solution.py:15
  104.8 7.3 %collective-permute-start.7 = (bf16[1,64,34,1]{1,2,3,0:T(8,128)(2,1)S(1)}, bf16[1,64,34,1]{1,2,3,0:T(8,128)(2,1)S(1)}, u32[]{:S(2)}, u32[]{:S(2)}) collective-permute-start(bf16[1,64,34,1]{1,2,3,0:T(8,128)(2,1)S(1)} %copy.41), channel_id=1, source_target_pairs={{0,1},{2,3},{4,5},{6,7},{8,9},{10,11},{12,13},{14,15},{16,17},{18,... | collective-permute-start | bytes 13064 | tf_op jit(solution)/shard_map/ppermute | solution.py:14
  116.0 2.5 %copy-start.10 = (f32[32,256,64]{1,2,0:T(8,128)S(1)}, f32[32,256,64]{1,2,0:T(8,128)}, u32[]{:S(2)}) copy-start(f32[32,256,64]{1,2,0:T(8,128)} %fusion.52) | copy-start | bytes 6291460
  (7 other events, 10.9 us)
Sparse Core Ops, SparseCore 0:
  101.8 23.6 reduce-scatter.1
where the time goes:
time: 163 us; the launch traced here: 162 us
  blocking collectives  70.7 us (43%)
  matrix products  31.1 us (19%)
  starting transfers between devices  21 us (13%)
  between operations  14.6 us (9%)
  local copies, waits for them, and re-layouts  13.5 us (8%)
  waiting for transfers between devices  6.31 us (4%)
  other arithmetic  5.31 us (3%)
    psum x1, blocking collectives, per_device(): lax.psum((local_pre, local_sq, local_cot, local_cross), ('dp', 'row', 'co...  40.6 us
    psum x1, blocking collectives, per_device(): spatial = lax.psum(local_kernel, ('row', 'col'))  30 us
    ppermute x4, starting transfers between devices, with_halo(): before = lax.ppermute(last, axis, up)  15.8 us
    dot_general x9, matrix products, per_device(): jnp.einsum('oc,bchw->bohw', kernel[tap_row, tap_col], window, preferred_e...  15.4 us
    unnamed x48, local copies, waits for them, and re-layouts  10.1 us
    dot_general x9, matrix products, per_device(): jnp.einsum('oc,bohw->bchw', kernel[tap_row, tap_col], shifted, preferred_...  9.7 us
    dot_general x9, matrix products, per_device(): jnp.einsum('bohw,bchw->oc', pre_grad, window, preferred_element_type=jnp....  5.99 us
    ppermute x4, starting transfers between devices, with_halo(): after = lax.ppermute(initial, axis, down)  5.16 us
  transfers between devices with their start and end apart: 9, of which 3 were waited for; matrix products, arithmetic and copies ran while one was open for 15% of the time, Pallas kernels for 0%

commit v1 on v0

--- a/solution.py
+++ b/solution.py
@@ -69,7 +69,8 @@
             )
     factor = total ** (-0.5)
     local_kernel = jnp.stack(kernel_terms).reshape(3, 3, channels, channels) * factor
-    spatial = lax.psum(local_kernel, ("row", "col"))
+    one_axis = lax.psum(local_kernel, "col")
+    spatial = lax.psum(one_axis, "row")
     weight_grad = lax.psum_scatter(spatial, "dp", scatter_dimension=2, tiled=True)
     return (input_grad.astype(jnp.bfloat16), weight_grad, sum_norm / total, sum_cot / total)
 

time: 163 us -> 158 us (0.969)
  blocking collectives: 70.7 us -> 65.3 us
    psum x1 -> x2, blocking collectives: 30 us -> 24.7 us  [the longest x1 20.5 us: per_device(): spatial = lax.psum(one_axis, 'row')]
  transfers between devices with their start and end apart: 9 -> 9, of which waited for: 3 -> 3; matrix products, arithmetic and copies ran while one was open for 15% -> 16% of each run, Pallas kernels for 0% -> 0%
where the time goes in v1:
time: 158 us; the launch traced here: 157 us
  blocking collectives  65.3 us (41%)
  matrix products  31.1 us (20%)
  starting transfers between devices  21 us (13%)
  between operations  14.6 us (9%)
  local copies, waits for them, and re-layouts  13.5 us (9%)
  waiting for transfers between devices  6.3 us (4%)
  other arithmetic  5.31 us (3%)
    psum x1, blocking collectives, per_device(): lax.psum((local_pre, local_sq, local_cot, local_cross), ('dp', 'row', 'co...  40.6 us
    psum x1, blocking collectives, per_device(): spatial = lax.psum(one_axis, 'row')  20.5 us
    ppermute x4, starting transfers between devices, with_halo(): before = lax.ppermute(last, axis, up)  15.8 us
    dot_general x9, matrix products, per_device(): jnp.einsum('oc,bchw->bohw', kernel[tap_row, tap_col], window, preferred_e...  15.4 us
    unnamed x48, local copies, waits for them, and re-layouts  10.1 us
    dot_general x9, matrix products, per_device(): jnp.einsum('oc,bohw->bchw', kernel[tap_row, tap_col], shifted, preferred_...  9.75 us
    dot_general x9, matrix products, per_device(): jnp.einsum('bohw,bchw->oc', pre_grad, window, preferred_element_type=jnp....  5.99 us
    ppermute x4, starting transfers between devices, with_halo(): after = lax.ppermute(initial, axis, down)  5.16 us
  transfers between devices with their start and end apart: 9, of which 3 were waited for; matrix products, arithmetic and copies ran while one was open for 16% of the time, Pallas kernels for 0%

profile of v1, /device:TPU:0, one launch (start us, length us, event | category | flops | bytes accessed | tf_op | source)
XLA Modules:
  0.0 157.1 jit_solution(1796639763252374554)
XLA Ops:
  7.2 1.9 %copy.26 = bf16[1,64,32,256]{3,1,2,0:T(8,128)(2,1)S(1)} copy(bf16[1,64,32,256]{3,2,1,0:T(8,128)(2,1)} %param.4) | data formatting | bytes 2097152 | tf_op args[0]
  9.2 5.0 %collective-permute-start = (bf16[1,64,1,256]{3,1,2,0:T(8,128)(2,1)S(1)}, bf16[1,64,1,256]{3,1,2,0:T(8,128)(2,1)S(1)}, u32[]{:S(2)}, u32[]{:S(2)}) collective-permute-start(bf16[1,64,1,256]{3,1,2,0:T(8,128)(2,1)S(1)} %get-tuple-element.29), channel_id=1, source_target_pairs={{0,2},{2,4},{4,6},{1,3},{3,5},{5,7},{8,10},{10,12},{12,14},{9,11},... | collective-permute-start | bytes 98312 | tf_op jit(solution)/shard_map/ppermute | solution.py:14
  15.4 2.2 %fusion.55 = f32[32,256,64]{1,2,0:T(8,128)} fusion(bf16[64,32,256]{2,1,0:T(8,128)(2,1)S(1)} %bitcast.222, bf16[3,3,64,64]{3,2,1,0:T(8,128)(2,1)S(1)} %copy-done.18), kind=kOutput, calls=%fused_computation.92 | convolution fusion | flops 67108864 | bytes 3162112 | tf_op jit(solution)/shard_map/oc,bchw->bohw/dot_general | solution.py:30
  18.3 1.7 %collective-permute-done.1 = bf16[1,64,1,256]{3,1,2,0:T(8,128)(2,1)S(1)} collective-permute-done((bf16[1,64,1,256]{3,1,2,0:T(8,128)(2,1)S(1)}, bf16[1,64,1,256]{3,1,2,0:T(8,128)(2,1)S(1)}, u32[]{:S(2)}, u32[]{:S(2)}) %collective-permute-start.1) | collective-permute-done | bytes 32800 | tf_op jit(solution)/shard_map/ppermute | solution.py:15
  22.2 3.0 %collective-permute-start.2 = (bf16[1,64,34,1]{1,2,3,0:T(8,128)(2,1)S(1)}, bf16[1,64,34,1]{1,2,3,0:T(8,128)(2,1)S(1)}, u32[]{:S(2)}, u32[]{:S(2)}) collective-permute-start(bf16[1,64,34,1]{1,2,3,0:T(8,128)(2,1)S(1)} %copy.29), channel_id=1, source_target_pairs={{0,1},{2,3},{4,5},{6,7},{8,9},{10,11},{12,13},{14,15},{16,17},{18,... | collective-permute-start | bytes 13064 | tf_op jit(solution)/shard_map/ppermute | solution.py:14
  25.2 1.8 %fusion.58 = f32[32,256,64]{1,2,0:T(8,128)} fusion(bf16[1,64,32,256]{3,1,2,0:T(8,128)(2,1)S(1)} %copy.26, bf16[1,64,1,256]{3,1,2,0:T(8,128)(2,1)S(1)} %collective-permute-done, bf16[3,3,64,64]{3,2,1,0:T(8,128)(2,1)S(1)} %copy-done.18), kind=kOutput, calls=%fused_computation.94 | convolution fusion | flops 69206016 | bytes 3194880 | tf_op jit(solution)/shard_map/oc,bchw->bohw/dot_general | solution.py:30
  27.0 1.7 %fusion.61 = f32[32,256,64]{1,2,0:T(8,128)} fusion(bf16[1,64,1,256]{3,1,2,0:T(8,128)(2,1)S(1)} %collective-permute-done.1, bf16[1,64,32,256]{3,1,2,0:T(8,128)(2,1)S(1)} %copy.26, bf16[3,3,64,64]{3,2,1,0:T(8,128)(2,1)S(1)} %copy-done.18), kind=kOutput, calls=%fused_computation.95 | convolution fusion | flops 69206016 | bytes 3194880 | tf_op jit(solution)/shard_map/oc,bchw->bohw/dot_general | solution.py:30
  29.1 2.0 %fusion.78 = f32[32,256,64]{1,2,0:T(8,128)} fusion(bf16[3,3,64,64]{3,2,1,0:T(8,128)(2,1)S(1)} %copy-done.18, bf16[1,64,34,256]{3,1,2,0:T(8,128)(2,1)S(1)} %constant_dynamic-update-slice_fusion, bf16[1,64,34,1]{3,1,2,0:T(8,128)(2,1)S(1)} %copy.33), kind=kOutput, calls=%fused_computation.109 | convolution fusion | flops 69206016 | bytes 3784704 | tf_op jit(solution)/shard_map/oc,bchw->bohw/dot_general | solution.py:30
  31.1 2.1 %fusion.86 = f32[32,256,64]{1,2,0:T(8,128)} fusion(bf16[3,3,64,64]{3,2,1,0:T(8,128)(2,1)S(1)} %copy-done.18, bf16[1,64,34,256]{3,1,2,0:T(8,128)(2,1)S(1)} %constant_dynamic-update-slice_fusion, bf16[1,64,34,1]{3,1,2,0:T(8,128)(2,1)S(1)} %copy.33), kind=kOutput, calls=%fused_computation.117 | convolution fusion | flops 69206016 | bytes 3784704 | tf_op jit(solution)/shard_map/oc,bchw->bohw/dot_general | solution.py:30
  38.3 3.8 %fusion.3 = (f32[64]{0:T(128)S(1)}, f32[64]{0:T(128)S(1)}, f32[64]{0:T(128)S(1)}, f32[32,256,64]{1,2,0:T(8,128)S(1)}) fusion(bf16[1,64,32,256]{3,2,1,0:T(8,128)(2,1)} %param.7, bf16[1,64,34,1]{3,1,2,0:T(8,128)(2,1)S(1)} %copy-done.2, bf16[1,64,34,256]{3,1,2,0:T(8,128)(2,1)S(1)} %constant_dynamic-update-slice_fusion, ...), kind=kOutput, calls=%fused_computation.6 | convolution fusion | flops 76545856 | bytes 21611264 | tf_op jit(solution)/shard_map/oc,bchw->bohw/dot_general | solution.py:30
  42.4 40.6 %all-reduce = (f32[64]{0:T(128)S(1)}, f32[64]{0:T(128)S(1)}, f32[64]{0:T(128)S(1)}, f32[64]{0:T(128)S(1)}) all-reduce(f32[64]{0:T(128)S(1)} %get-tuple-element.13, f32[64]{0:T(128)S(1)} %reduce_sum.37, f32[64]{0:T(128)S(1)} %get-tuple-element.12, f32[64]{0:T(128)S(1)} %get-tuple-element.14), channel_id=1, replica_groups=mesh['dp'=4,'row'=4,'col'=2] {'dp','row','col'}, use_global_device_ids=true, to_apply=%region_1.0 | all-reduce | flops 256 | bytes 2048 | tf_op jit(solution)/shard_map/psum | solution.py:41
  83.1 2.8 %fusion.2 = bf16[1,64,32,256]{3,1,2,0:T(8,128)(2,1)S(1)} fusion(f32[32,256,64]{1,2,0:T(8,128)} %copy-done, f32[64]{0:T(128)S(1)} %get-tuple-element.32, f32[64]{0:T(128)S(1)} %get-tuple-element.20, f32[64]{0:T(128)S(1)} %get-tuple-element.33, f32[64]{0:T(128)S(1)} %get-tuple-element.31, f32[64]{0:T(128)S(1)} %get-tuple-element.19, ...), kind=kLoop, calls=%fused_computation.5 | loop fusion | flops 4194304 | bytes 4195584 | tf_op jit(solution)/shard_map/convert_element_type | solution.py:51
  86.5 1.8 %fusion.52 = f32[32,256,64]{1,2,0:T(8,128)} fusion(bf16[1,64,32,256]{3,1,2,0:T(8,128)(2,1)S(1)} %fusion.2, bf16[3,3,64,64]{3,2,1,0:T(8,128)(2,1)S(1)} %copy-done.18), kind=kOutput, calls=%fused_computation.89 | convolution fusion | flops 67108864 | bytes 3162112 | tf_op jit(solution)/shard_map/oc,bohw->bchw/dot_general | solution.py:60
  91.3 1.3 fusion.11
  96.3 4.5 %collective-permute-start.4 = (bf16[1,64,1,256]{3,1,2,0:T(8,128)(2,1)S(1)}, bf16[1,64,1,256]{3,1,2,0:T(8,128)(2,1)S(1)}, u32[]{:S(2)}, u32[]{:S(2)}) collective-permute-start(bf16[1,64,1,256]{3,1,2,0:T(8,128)(2,1)S(1)} %get-tuple-element.28), channel_id=1, source_target_pairs={{0,2},{2,4},{4,6},{1,3},{3,5},{5,7},{8,10},{10,12},{12,14},{9,11},... | collective-permute-start | bytes 98312 | tf_op jit(solution)/shard_map/ppermute | solution.py:14
  104.8 3.2 %collective-permute-start.7 = (bf16[1,64,34,1]{1,2,3,0:T(8,128)(2,1)S(1)}, bf16[1,64,34,1]{1,2,3,0:T(8,128)(2,1)S(1)}, u32[]{:S(2)}, u32[]{:S(2)}) collective-permute-start(bf16[1,64,34,1]{1,2,3,0:T(8,128)(2,1)S(1)} %copy.41), channel_id=1, source_target_pairs={{0,1},{2,3},{4,5},{6,7},{8,9},{10,11},{12,13},{14,15},{16,17},{18,... | collective-permute-start | bytes 13064 | tf_op jit(solution)/shard_map/ppermute | solution.py:14
  108.1 1.9 %fusion.35 = f32[32,256,64]{1,2,0:T(8,128)} fusion(bf16[1,64,1,256]{3,1,2,0:T(8,128)(2,1)S(1)} %collective-permute-done.5, bf16[1,64,32,256]{3,1,2,0:T(8,128)(2,1)S(1)} %fusion.2, bf16[3,3,64,64]{3,2,1,0:T(8,128)(2,1)S(1)} %copy-done.18), kind=kOutput, calls=%fused_computation.68 | convolution fusion | flops 67633152 | bytes 3194880 | tf_op jit(solution)/shard_map/oc,bohw->bchw/dot_general | solution.py:60
  109.9 1.8 %fusion.27 = f32[32,256,64]{1,2,0:T(8,128)} fusion(bf16[1,64,32,256]{3,1,2,0:T(8,128)(2,1)S(1)} %fusion.2, bf16[1,64,1,256]{3,1,2,0:T(8,128)(2,1)S(1)} %collective-permute-done.4, bf16[3,3,64,64]{3,2,1,0:T(8,128)(2,1)S(1)} %copy-done.18), kind=kOutput, calls=%fused_computation.56 | convolution fusion | flops 67633152 | bytes 3194880 | tf_op jit(solution)/shard_map/oc,bohw->bchw/dot_general | solution.py:60
  112.5 1.4 maximum_maximum_fusion
  118.5 1.6 %fusion.24 = bf16[1,64,32,256]{3,1,2,0:T(8,128)(2,1)S(1)} fusion(f32[32,256,64]{1,2,0:T(8,128)S(1)} %copy-done.13, f32[32,256,64]{1,2,0:T(8,128)S(1)} %fusion.30, f32[32,256,64]{1,2,0:T(8,128)S(1)} %fusion.31, f32[32,256,64]{1,2,0:T(8,128)S(1)} %copy-done.10, f32[32,256,64]{1,2,0:T(8,128)S(1)} %fusion.32, f32[32,256,64]{1,2,0:T(8,128)S(1)} %fusion.33, ...), kind=kOutput, calls=%fused_computation.51 | convolution fusion | flops 71827456 | bytes 18890752 | tf_op jit(solution)/shard_map/oc,bohw->bchw/dot_general | solution.py:60
  120.1 1.6 copy.51
  121.7 3.8 %reduce-scatter.2.cloned.1.call-done = f32[3,3,16,64]{3,2,1,0:T(8,128)} async-done(((f32[3,3,64,64]{3,2,1,0:T(8,128)}), f32[3,3,16,64]{3,2,1,0:T(8,128)}) %reduce-scatter.2.cloned.1.call-update) | async-done | bytes 36880 | tf_op jit(solution)/shard_map/reduce_scatter | solution.py:74
  125.5 4.2 %psum.49 = f32[3,3,16,64]{3,2,1,0:T(8,128)S(1)} all-reduce(f32[3,3,16,64]{3,2,1,0:T(8,128)} %reduce-scatter.2.cloned.1.call-done), channel_id=1, replica_groups=mesh['dp'=4,'row'=4,'col'=2] {'col'}, use_global_device_ids=true, to_apply=%region_8.0 | all-reduce | flops 9216 | bytes 73728 | tf_op jit(solution)/shard_map/psum | solution.py:72
  129.7 20.5 %psum.48 = f32[3,3,16,64]{3,2,1,0:T(8,128)} all-reduce(f32[3,3,16,64]{3,2,1,0:T(8,128)S(1)} %psum.49), channel_id=1, replica_groups=mesh['dp'=4,'row'=4,'col'=2] {'row'}, use_global_device_ids=true, to_apply=%region_9.0 | all-reduce | flops 9216 | bytes 73728 | tf_op jit(solution)/shard_map/psum | solution.py:73
  (93 shorter events, 26.2 us)
Async XLA Ops:
  7.2 8.3 %copy-start.8 = (bf16[1,64,32,256]{3,2,1,0:T(8,128)(2,1)S(1)}, bf16[1,64,32,256]{3,2,1,0:T(8,128)(2,1)}, u32[]{:S(2)}) copy-start(bf16[1,64,32,256]{3,2,1,0:T(8,128)(2,1)} %param.4) | copy-start | bytes 3145732
  7.2 8.3 %copy-start.18 = (bf16[3,3,64,64]{3,2,1,0:T(8,128)(2,1)S(1)}, bf16[3,3,64,64]{3,2,1,0:T(8,128)(2,1)}, u32[]{:S(2)}) copy-start(bf16[3,3,64,64]{3,2,1,0:T(8,128)(2,1)} %param.5) | copy-start | bytes 221188
  7.2 118.3 %reduce-scatter.2.cloned.1.call-start = ((), (), s32[]{:S(2)}) async-start(), calls=%async_computation.1 | async-start | bytes 368640 | tf_op jit(solution)/shard_map/reduce_scatter | solution.py:74
  9.1 17.8 %copy-start.6 = (bf16[1,64,32,256]{3,1,2,0:T(8,128)(2,1)}, bf16[1,64,32,256]{3,1,2,0:T(8,128)(2,1)S(1)}, u32[]{:S(2)}) copy-start(bf16[1,64,32,256]{3,1,2,0:T(8,128)(2,1)S(1)} %copy.26) | copy-start | bytes 3145732
  9.2 8.5 %collective-permute-start = (bf16[1,64,1,256]{3,1,2,0:T(8,128)(2,1)S(1)}, bf16[1,64,1,256]{3,1,2,0:T(8,128)(2,1)S(1)}, u32[]{:S(2)}, u32[]{:S(2)}) collective-permute-start(bf16[1,64,1,256]{3,1,2,0:T(8,128)(2,1)S(1)} %get-tuple-element.29), channel_id=1, source_target_pairs={{0,2},{2,4},{4,6},{1,3},{3,5},{5,7},{8,10},{10,12},{12,14},{9,11},... | collective-permute-start | bytes 98312 | tf_op jit(solution)/shard_map/ppermute | solution.py:14
  14.1 5.8 %collective-permute-start.1 = (bf16[1,64,1,256]{3,1,2,0:T(8,128)(2,1)S(1)}, bf16[1,64,1,256]{3,1,2,0:T(8,128)(2,1)S(1)}, u32[]{:S(2)}, u32[]{:S(2)}) collective-permute-start(bf16[1,64,1,256]{3,1,2,0:T(8,128)(2,1)S(1)} %get-tuple-element.30), channel_id=1, source_target_pairs={{2,0},{4,2},{6,4},{3,1},{5,3},{7,5},{10,8},{12,10},{14,12},{11,9},... | collective-permute-start | bytes 98312 | tf_op jit(solution)/shard_map/ppermute | solution.py:15
  20.6 8.2 %collective-permute-start.3 = (bf16[1,64,34,1]{1,2,3,0:T(8,128)(2,1)S(1)}, bf16[1,64,34,1]{1,2,3,0:T(8,128)(2,1)S(1)}, u32[]{:S(2)}, u32[]{:S(2)}) collective-permute-start(bf16[1,64,34,1]{1,2,3,0:T(8,128)(2,1)S(1)} %copy.32), channel_id=1, source_target_pairs={{1,0},{3,2},{5,4},{7,6},{9,8},{11,10},{13,12},{15,14},{17,16},{19,... | collective-permute-start | bytes 13064 | tf_op jit(solution)/shard_map/ppermute | solution.py:15
  22.2 11.1 %collective-permute-start.2 = (bf16[1,64,34,1]{1,2,3,0:T(8,128)(2,1)S(1)}, bf16[1,64,34,1]{1,2,3,0:T(8,128)(2,1)S(1)}, u32[]{:S(2)}, u32[]{:S(2)}) collective-permute-start(bf16[1,64,34,1]{1,2,3,0:T(8,128)(2,1)S(1)} %copy.29), channel_id=1, source_target_pairs={{0,1},{2,3},{4,5},{6,7},{8,9},{10,11},{12,13},{14,15},{16,17},{18,... | collective-permute-start | bytes 13064 | tf_op jit(solution)/shard_map/ppermute | solution.py:14
  29.1 4.1 %copy-start.1 = (bf16[1,64,34,1]{3,1,2,0:T(8,128)(2,1)}, bf16[1,64,34,1]{3,1,2,0:T(8,128)(2,1)S(1)}, u32[]{:S(2)}) copy-start(bf16[1,64,34,1]{3,1,2,0:T(8,128)(2,1)S(1)} %copy.33) | copy-start | bytes 13060
  33.6 2.4 %copy-start.17 = (f32[32,256,64]{1,2,0:T(8,128)S(1)}, f32[32,256,64]{1,2,0:T(8,128)}, u32[]{:S(2)}) copy-start(f32[32,256,64]{1,2,0:T(8,128)} %fusion.86) | copy-start | bytes 6291460
  34.2 2.6 %copy-start.14 = (f32[32,256,64]{1,2,0:T(8,128)S(1)}, f32[32,256,64]{1,2,0:T(8,128)}, u32[]{:S(2)}) copy-start(f32[32,256,64]{1,2,0:T(8,128)} %fusion.58) | copy-start | bytes 6291460
  34.2 3.2 %copy-start.15 = (f32[32,256,64]{1,2,0:T(8,128)S(1)}, f32[32,256,64]{1,2,0:T(8,128)}, u32[]{:S(2)}) copy-start(f32[32,256,64]{1,2,0:T(8,128)} %fusion.61) | copy-start | bytes 6291460
  34.8 2.7 %copy-start.2 = (bf16[1,64,34,1]{3,1,2,0:T(8,128)(2,1)S(1)}, bf16[1,64,34,1]{3,1,2,0:T(8,128)(2,1)}, u32[]{:S(2)}) copy-start(bf16[1,64,34,1]{3,1,2,0:T(8,128)(2,1)} %copy-done.1) | copy-start | bytes 13060
  34.8 3.5 %copy-start.11 = (f32[32,256,64]{1,2,0:T(8,128)S(1)}, f32[32,256,64]{1,2,0:T(8,128)}, u32[]{:S(2)}) copy-start(f32[32,256,64]{1,2,0:T(8,128)} %fusion.55) | copy-start | bytes 6291460
  42.1 40.9 %copy-start = (f32[32,256,64]{1,2,0:T(8,128)}, f32[32,256,64]{1,2,0:T(8,128)S(1)}, u32[]{:S(2)}) copy-start(f32[32,256,64]{1,2,0:T(8,128)S(1)} %get-tuple-element.34) | copy-start | bytes 6291460
  42.1 40.9 %copy-start.21 = (f32[64]{0:T(128)S(1)}, f32[64]{0:T(128)}, u32[]{:S(2)}) copy-start(f32[64]{0:T(128)} %param.6) | copy-start | bytes 772
  83.0 2.8 %copy-start.19 = (f32[64]{0:T(128)}, f32[64]{0:T(128)S(1)}, u32[]{:S(2)}) copy-start(f32[64]{0:T(128)S(1)} %get-tuple-element.31) | copy-start | bytes 772
  83.0 2.8 %copy-start.20 = (f32[64]{0:T(128)}, f32[64]{0:T(128)S(1)}, u32[]{:S(2)}) copy-start(f32[64]{0:T(128)S(1)} %get-tuple-element.32) | copy-start | bytes 772
  83.0 2.8 %copy-start.5 = (bf16[1,64,34,1]{3,1,2,0:T(8,128)(2,1)S(1)}, bf16[1,64,34,1]{3,1,2,0:T(8,128)(2,1)}, u32[]{:S(2)}) copy-start(bf16[1,64,34,1]{3,1,2,0:T(8,128)(2,1)} %copy-done.4) | copy-start | bytes 13060
  95.0 6.6 %collective-permute-start.5 = (bf16[1,64,1,256]{3,1,2,0:T(8,128)(2,1)S(1)}, bf16[1,64,1,256]{3,1,2,0:T(8,128)(2,1)S(1)}, u32[]{:S(2)}, u32[]{:S(2)}) collective-permute-start(bf16[1,64,1,256]{3,1,2,0:T(8,128)(2,1)S(1)} %get-tuple-element.27), channel_id=1, source_target_pairs={{2,0},{4,2},{6,4},{3,1},{5,3},{7,5},{10,8},{12,10},{14,12},{11,9},... | collective-permute-start | bytes 98312 | tf_op jit(solution)/shard_map/ppermute | solution.py:15
  96.3 6.1 %collective-permute-start.4 = (bf16[1,64,1,256]{3,1,2,0:T(8,128)(2,1)S(1)}, bf16[1,64,1,256]{3,1,2,0:T(8,128)(2,1)S(1)}, u32[]{:S(2)}, u32[]{:S(2)}) collective-permute-start(bf16[1,64,1,256]{3,1,2,0:T(8,128)(2,1)S(1)} %get-tuple-element.28), channel_id=1, source_target_pairs={{0,2},{2,4},{4,6},{1,3},{3,5},{5,7},{8,10},{10,12},{12,14},{9,11},... | collective-permute-start | bytes 98312 | tf_op jit(solution)/shard_map/ppermute | solution.py:14
  103.2 8.5 %collective-permute-start.6 = (bf16[1,64,34,1]{1,2,3,0:T(8,128)(2,1)S(1)}, bf16[1,64,34,1]{1,2,3,0:T(8,128)(2,1)S(1)}, u32[]{:S(2)}, u32[]{:S(2)}) collective-permute-start(bf16[1,64,34,1]{1,2,3,0:T(8,128)(2,1)S(1)} %copy.37), channel_id=1, source_target_pairs={{1,0},{3,2},{5,4},{7,6},{9,8},{11,10},{13,12},{15,14},{17,16},{19,... | collective-permute-start | bytes 13064 | tf_op jit(solution)/shard_map/ppermute | solution.py:15
  104.8 7.3 %collective-permute-start.7 = (bf16[1,64,34,1]{1,2,3,0:T(8,128)(2,1)S(1)}, bf16[1,64,34,1]{1,2,3,0:T(8,128)(2,1)S(1)}, u32[]{:S(2)}, u32[]{:S(2)}) collective-permute-start(bf16[1,64,34,1]{1,2,3,0:T(8,128)(2,1)S(1)} %copy.41), channel_id=1, source_target_pairs={{0,1},{2,3},{4,5},{6,7},{8,9},{10,11},{12,13},{14,15},{16,17},{18,... | collective-permute-start | bytes 13064 | tf_op jit(solution)/shard_map/ppermute | solution.py:14
  116.1 2.5 %copy-start.10 = (f32[32,256,64]{1,2,0:T(8,128)S(1)}, f32[32,256,64]{1,2,0:T(8,128)}, u32[]{:S(2)}) copy-start(f32[32,256,64]{1,2,0:T(8,128)} %fusion.52) | copy-start | bytes 6291460
  (7 other events, 10.9 us)
Sparse Core Ops, SparseCore 0:
  101.8 23.6 reduce-scatter.1
